TPU v7x, 32 devices: a whole 2x2x4 slice. The times are simulated.
32 devices in a mesh: dp: 16 (over z, x, core), tensor: 2 (over y).
Axes of the slice: x: 2, y: 2, z: 4, core: 2. Of those that a mesh axis runs over, the one named last changes fastest.
Arguments:
- hidden: bfloat16 [5120, 18432], P('dp', 'tensor'), may hold values from -6 to 6
- fixed_down_weight: bfloat16 [18432, 4608], P('tensor', 'dp'), may hold values from -4 to 4
- lowrank_factor_b: bfloat16 [18432, 16], P('tensor'), may hold values from -0.046875 to 0.046875
- lowrank_factor_a: bfloat16 [16, 4608], P(None, 'dp'), may hold values from -1.5 to 1.5
- magnitude: float32 [4608], P('tensor'), may hold values from 0.5 to 2
- cotangent: bfloat16 [5120, 4608], P('dp', 'tensor'), may hold values from -0.083496094 to 0.083496094
Outputs:
- mixed: bfloat16 [5120, 4608], P('dp', 'tensor')
- gradient_column_scale: float32 [4608], P(('tensor', 'dp'))
- gradient_factor_a: float32 [16, 4608], P(None, ('tensor', 'dp'))
- gradient_factor_b: float32 [18432, 16], P(('tensor', 'dp'))
All inputs are finite; a program needn't handle non-finite values.
Results may differ from a plain program's by a relative error of at most 0.0054.
Values may be sent and summed in bfloat16 or wider, within the bound.
No kernel may reach another device: no remote copies, remote signals or barrier semaphores. Data moves between devices by JAX's collectives and lax.ppermute only.
A program may use at most 192 MiB of HBM per device.

v0:
```python
import jax
import jax.numpy as jnp
from jax import lax
from jax.sharding import PartitionSpec as P


def body(hidden, fixed_down_weight, lowrank_factor_b, lowrank_factor_a, magnitude, cotangent):
    out_cols = magnitude.shape[0]
    own = lax.axis_index("tensor")
    lowrank_portion = jnp.dot(hidden, lowrank_factor_b, preferred_element_type=jnp.float32)
    combined_weight = fixed_down_weight.astype(jnp.float32) + jnp.dot(
        lowrank_factor_b, lowrank_factor_a, preferred_element_type=jnp.float32
    )
    local_sq = jnp.sum(combined_weight * combined_weight, axis=0)
    low_full, block_sq = lax.psum((lowrank_portion, local_sq), "tensor")
    col_sq = lax.all_gather(block_sq, "dp", axis=0, tiled=True)
    sq_len = 1
    weight_shape = (1, 1)
    squares = jnp.zeros((sq_len,), jnp.float32)
    full_w = jnp.zeros(weight_shape, jnp.bfloat16)
    w_piece = lax.all_gather(fixed_down_weight, "dp", axis=1, tiled=True)
    factor_a_slice = lax.all_gather(lowrank_factor_a, "dp", axis=1, tiled=True)
    products = jnp.dot(hidden, w_piece, preferred_element_type=jnp.float32)
    full_a = factor_a_slice
    products, squares, full_a, full_w = (products, squares, full_a, full_w)
    column_norm_values = jnp.sqrt(col_sq + 1e-06)
    own_norms = lax.dynamic_slice_in_dim(column_norm_values, own * out_cols, out_cols, 0)
    scale = magnitude / own_norms
    lowrank_block_update = low_full.astype(jnp.bfloat16)
    summed = lax.psum_scatter(products, "tensor", scatter_dimension=1, tiled=True)
    own_a = lax.dynamic_slice_in_dim(full_a, own * out_cols, out_cols, 1)
    prenorm_output = summed + jnp.dot(
        lowrank_block_update, own_a, preferred_element_type=jnp.float32
    )
    mixed = (prenorm_output * scale).astype(jnp.bfloat16)
    cot = cotangent.astype(jnp.float32)
    mag_part = jnp.sum(cot * prenorm_output, axis=0) / own_norms
    prenorm_gradient_b = (cot * scale).astype(jnp.bfloat16)
    factor_a_portion = jnp.dot(
        lowrank_block_update.T, prenorm_gradient_b, preferred_element_type=jnp.float32
    )
    back_part = jnp.dot(prenorm_gradient_b, own_a.T, preferred_element_type=jnp.float32)
    backward_factor_b = lax.psum(back_part, "tensor").astype(jnp.bfloat16)
    b_part = jnp.dot(hidden.T, backward_factor_b, preferred_element_type=jnp.float32)
    gradient_column_scale, gradient_factor_b = (
        lax.psum_scatter(mag_part, "dp", scatter_dimension=0, tiled=True),
        lax.psum_scatter(b_part, "dp", scatter_dimension=0, tiled=True),
    )
    gradient_factor_a = lax.psum_scatter(factor_a_portion, "dp", scatter_dimension=1, tiled=True)
    return (mixed, gradient_column_scale, gradient_factor_a, gradient_factor_b)


def solution(mesh):
    return jax.shard_map(
        body,
        mesh=mesh,
        in_specs=(
            P("dp", "tensor"),
            P("tensor", "dp"),
            P("tensor", None),
            P(None, "dp"),
            P("tensor"),
            P("dp", "tensor"),
        ),
        out_specs=(
            P("dp", "tensor"),
            P(("tensor", "dp")),
            P(None, ("tensor", "dp")),
            P(("tensor", "dp"), None),
        ),
        check_vma=False,
    )
```

profile of v0, /device:TPU:0, one launch (start us, length us, event | category | flops | bytes accessed | tf_op | source)
XLA Modules:
  0.0 711.5 jit_solution(8600215113139559798)
XLA Ops:
  7.2 0.0 copy-start
  7.2 0.0 copy-start.4
  7.2 0.0 copy-start.2
  7.2 0.0 all-gather.3.cloned.1.call-start
  7.2 0.7 all-gather.3.cloned.1.call-update
  7.9 0.0 reduce-scatter.10.cloned.1.call-start
  8.0 0.0 copy-done.2
  8.0 24.5 %all-gather = bf16[16,288,16]{1,2,0:T(8,128)(2,1)S(1)} all-gather(bf16[1,288,16]{1,2,0:T(8,128)(2,1)S(1)} %bitcast.24), channel_id=1, replica_groups=mesh['dp'=16,'tensor'=2] {'dp'}, dimensions={0}, use_global_device_ids=true | all-gather | bytes 156672 | tf_op jit(solution)/shard_map/all_gather | solution.py:22
  32.6 0.2 reshape.13
  32.8 0.0 copy-done.4
  32.8 0.6 fusion.17
  34.0 0.0 copy-done
  34.0 0.0 copy-start.3
  34.0 0.0 copy-start.1
  34.1 4.4 fusion.3
  38.4 4.9 psum.22
  43.4 0.2 dynamic-update-slice
  43.6 61.0 %all-reduce = f32[4608]{0:T(1024)S(1)} all-reduce(f32[4608]{0:T(1024)S(1)} %dynamic-update-slice), channel_id=1, replica_groups=mesh['dp'=16,'tensor'=2] {'dp'}, use_global_device_ids=true, to_apply=%add | all-reduce | flops 4608 | bytes 36864
  104.6 0.0 copy-done.3
  104.6 0.1 fusion.11
  104.7 0.0 copy-done.1
  104.7 0.5 fusion.4
  105.2 4.3 fusion.19
  109.6 8.7 %all-reduce.2 = (bf16[320,16]{0,1:T(8,128)(2,1)S(1)}, bf16[320,16]{0,1:T(8,128)(2,1)S(1)}) all-reduce(f32[320,16]{0,1:T(8,128)S(1)} %fusion.19, f32[320,16]{0,1:T(8,128)S(1)} %fusion.4), channel_id=1, replica_groups=mesh['dp'=16,'tensor'=2] {'tensor'}, use_global_device_ids=true, to_apply=%region_1.0 | all-reduce | flops 10240 | bytes 61440 | tf_op jit(solution)/shard_map/psum | solution.py:15
  118.3 1.8 convolution_bitcast_fusion.1
  120.1 0.0 reduce-scatter.10.cloned.1.call-update
  120.1 0.0 reduce-scatter.12.cloned.1.call-start
  120.2 3.7 convolution_bitcast_fusion
  123.9 2.9 copy.14
  126.8 0.0 reduce-scatter.12.cloned.1.call-update
  126.8 0.0 reduce-scatter.8.cloned.1.call-start
  126.8 296.7 %all-gather.3.cloned.1.call-done = bf16[9216,4608]{0,1:T(8,128)(2,1)} async-done(((bf16[9216,288]{0,1:T(8,128)(2,1)}), bf16[9216,4608]{0,1:T(8,128)(2,1)}) %all-gather.3.cloned.1.call-update) | async-done | bytes 84934672 | tf_op jit(solution)/shard_map/all_gather | solution.py:21
  423.6 40.2 %fusion.18 = f32[320,4608]{1,0:T(8,128)} fusion(bf16[320,9216]{1,0:T(8,128)(2,1)} %param.6, bf16[9216,4608]{0,1:T(8,128)(2,1)} %all-gather.3.cloned.1.call-done), kind=kOutput, calls=%fused_computation.24 | convolution fusion | flops 27179089920 | bytes 96731136 | tf_op jit(solution)/shard_map/dot_general | solution.py:23
  463.8 0.0 reduce-scatter.8.cloned.1.call-update
  464.4 22.3 %reduce-scatter.10.cloned.1.call-done = f32[144,16]{1,0:T(8,128)} async-done(((f32[2304,16]{1,0:T(8,128)}), f32[144,16]{1,0:T(8,128)}) %reduce-scatter.10.cloned.1.call-update) | async-done | bytes 9232
  486.7 1.6 copy.13
  488.3 77.0 %reduce-scatter.12.cloned.1.call-done = f32[576,16]{1,0:T(8,128)} async-done(((f32[9216,16]{1,0:T(8,128)}), f32[576,16]{1,0:T(8,128)}) %reduce-scatter.12.cloned.1.call-update) | async-done | bytes 36880
  565.2 1.7 copy.15
  566.9 72.6 %reduce-scatter.8.cloned.1.call-done = f32[320,2304]{1,0:T(8,128)} async-done(((f32[320,4608]{1,0:T(8,128)}), f32[320,2304]{1,0:T(8,128)}) %reduce-scatter.8.cloned.1.call-update) | async-done | bytes 2949136 | tf_op jit(solution)/shard_map/reduce_scatter | solution.py:30
  639.6 3.7 fusion.1
  643.3 0.1 fusion.12
  643.3 61.0 %all-reduce.1 = f32[2304]{0:T(1024)S(1)} all-reduce(f32[2304]{0:T(1024)S(1)} %fusion.12), channel_id=3, replica_groups=mesh['dp'=16,'tensor'=2] {'dp'}, use_global_device_ids=true, to_apply=%region_5.0.clone | all-reduce | flops 2304 | bytes 18432
  704.4 0.6 dynamic-slice.3
  (2 shorter events, 0.0 us)
Async XLA Ops:
  7.2 26.9 %copy-start = (bf16[9216,16]{0,1:T(8,128)(2,1)S(1)}, bf16[9216,16]{0,1:T(8,128)(2,1)}, u32[]{:S(2)}) copy-start(bf16[9216,16]{0,1:T(8,128)(2,1)} %param.8) | copy-start | bytes 884740
  7.2 25.6 %copy-start.4 = (u32[32]{0:T(128)S(1)}, u32[32]{0:T(128)}, u32[]{:S(2)}) copy-start(u32[32]{0:T(128)} %constant.16) | copy-start | bytes 388
  7.2 0.8 copy-start.2
  7.2 416.4 %all-gather.3.cloned.1.call-start = ((), (), s32[]{:S(2)}) async-start(), calls=%async_computation.3 | async-start | bytes 90243072 | tf_op jit(solution)/shard_map/all_gather | solution.py:21
  7.9 478.8 %reduce-scatter.10.cloned.1.call-start = ((), (), s32[]{:S(2)}) async-start(), calls=%async_computation.5 | async-start | bytes 1253376
  34.0 70.6 %copy-start.3 = (f32[2304]{0:T(1024)S(1)}, f32[2304]{0:T(1024)}, u32[]{:S(2)}) copy-start(f32[2304]{0:T(1024)} %param.10) | copy-start | bytes 27652
  34.0 70.7 %copy-start.1 = (bf16[320,2304]{1,0:T(8,128)(2,1)S(1)}, bf16[320,2304]{1,0:T(8,128)(2,1)}, u32[]{:S(2)}) copy-start(bf16[320,2304]{1,0:T(8,128)(2,1)} %param.11) | copy-start | bytes 4423684
  120.1 445.1 %reduce-scatter.12.cloned.1.call-start = ((), (), s32[]{:S(2)}) async-start(), calls=%async_computation.6 | async-start | bytes 5013504
  126.8 512.8 %reduce-scatter.8.cloned.1.call-start = ((), (), s32[]{:S(2)}) async-start(), calls=%async_computation.4 | async-start | bytes 8847360 | tf_op jit(solution)/shard_map/reduce_scatter | solution.py:30
Sparse Core Ops, SparseCore 0:
  9.6 413.9 all-gather.2
  427.7 58.9 reduce-scatter.9
  490.6 74.6 reduce-scatter.11
  567.4 72.1 reduce-scatter.7
where the time goes:
time: 712 us
  waiting for transfers between devices  469 us (66%)
  blocking collectives  160 us (22%)
  matrix products  58.6 us (8%)
  between operations  15.2 us (2%)
  local copies, waits for them, and re-layouts  7.9 us (1%)
    all_gather x1, waiting for transfers between devices, body(): w_piece = lax.all_gather(fixed_down_weight, 'dp', axis=1, tiled=True)  297 us
    unnamed x2, blocking collectives  122 us
    unnamed x6, waiting for transfers between devices  100 us
    reduce_scatter x1, waiting for transfers between devices, body(): lax.psum_scatter(products, 'tensor', scatter_dimension=1, tiled=True)  72.6 us
    dot_general x1, matrix products, body(): products = jnp.dot(hidden, w_piece, preferred_element_type=jnp.float32)  40.2 us
    all_gather x1, blocking collectives, body(): factor_a_slice = lax.all_gather(lowrank_factor_a, 'dp', axis=1, tiled=True)  24.5 us
  transfers between devices with their start and end apart: 4, of which 4 were waited for; matrix products, arithmetic and copies ran while one was open for 9% of the time, Pallas kernels for 0%

commit v1 on v0

--- a/solution.py
+++ b/solution.py
@@ -18,7 +18,7 @@
     weight_shape = (1, 1)
     squares = jnp.zeros((sq_len,), jnp.float32)
     full_w = jnp.zeros(weight_shape, jnp.bfloat16)
-    w_piece = lax.all_gather(fixed_down_weight, "dp", axis=1, tiled=True)
+    w_piece = jnp.concatenate(lax.all_gather(fixed_down_weight, "dp"), axis=1)
     factor_a_slice = lax.all_gather(lowrank_factor_a, "dp", axis=1, tiled=True)
     products = jnp.dot(hidden, w_piece, preferred_element_type=jnp.float32)
     full_a = factor_a_slice

time: 712 us -> 721 us (1.013)
  local copies, waits for them, and re-layouts: 7.9 us -> 121 us
  waiting for transfers between devices: 469 us -> 368 us
    unnamed x6, waiting for transfers between devices: 100 us -> 0.75 us
    reshape x0 -> x1, local copies, waits for them, and re-layouts: none -> 56.8 us  [body(): w_piece = jnp.concatenate(lax.all_gather(fixed_down_weight, 'dp'), axis=1)]
    unnamed x18 -> x41, local copies, waits for them, and re-layouts: 7.86 us -> 64.5 us
  transfers between devices with their start and end apart: 4 -> 4, of which waited for: 4 -> 2; matrix products, arithmetic and copies ran while one was open for 9% -> 24% of each run, Pallas kernels for 0% -> 0%
where the time goes in v1:
time: 721 us
  waiting for transfers between devices  368 us (51%)
  blocking collectives  160 us (22%)
  local copies, waits for them, and re-layouts  121 us (17%)
  matrix products  55.9 us (8%)
  between operations  15.4 us (2%)
    all_gather x1, waiting for transfers between devices, body(): w_piece = jnp.concatenate(lax.all_gather(fixed_down_weight, 'dp'), axis=1)  296 us
    unnamed x2, blocking collectives  122 us
    reduce_scatter x1, waiting for transfers between devices, body(): lax.psum_scatter(products, 'tensor', scatter_dimension=1, tiled=True)  70.4 us
    unnamed x41, local copies, waits for them, and re-layouts  64.5 us
    reshape x1, local copies, waits for them, and re-layouts, body(): w_piece = jnp.concatenate(lax.all_gather(fixed_down_weight, 'dp'), axis=1)  56.8 us
    dot_general x1, matrix products, body(): products = jnp.dot(hidden, w_piece, preferred_element_type=jnp.float32)  37.5 us
    all_gather x1, blocking collectives, body(): factor_a_slice = lax.all_gather(lowrank_factor_a, 'dp', axis=1, tiled=True)  24.5 us
  transfers between devices with their start and end apart: 4, of which 2 were waited for; matrix products, arithmetic and copies ran while one was open for 24% of the time, Pallas kernels for 0%

profile of v1, /device:TPU:0, one launch (start us, length us, event | category | flops | bytes accessed | tf_op | source)
XLA Modules:
  0.0 720.9 jit_solution(7452878573167720599)
XLA Ops:
  7.2 0.0 copy-start
  7.2 0.0 copy-start.13
  7.2 0.0 copy-start.11
  7.2 0.0 all-gather.4.cloned.1.call-start
  7.2 0.7 all-gather.4.cloned.1.call-update
  7.9 0.0 reduce-scatter.10.cloned.1.call-start
  8.0 0.0 copy-done.11
  8.0 24.5 %all-gather.1 = bf16[16,288,16]{1,2,0:T(8,128)(2,1)S(1)} all-gather(bf16[1,288,16]{1,2,0:T(8,128)(2,1)S(1)} %bitcast.33), channel_id=1, replica_groups=mesh['dp'=16,'tensor'=2] {'dp'}, dimensions={0}, use_global_device_ids=true | all-gather | bytes 156672 | tf_op jit(solution)/shard_map/all_gather | solution.py:22
  32.6 0.2 reshape.22
  32.8 0.0 copy-start.3
  32.8 0.0 copy-done.13
  32.8 0.6 fusion.17
  34.0 0.0 copy-done
  34.0 0.0 copy-start.12
  34.1 0.0 copy-start.1
  34.1 4.4 fusion.3
  38.4 4.9 psum.22
  43.4 0.2 dynamic-update-slice
  43.6 61.0 %all-reduce = f32[4608]{0:T(1024)S(1)} all-reduce(f32[4608]{0:T(1024)S(1)} %dynamic-update-slice), channel_id=1, replica_groups=mesh['dp'=16,'tensor'=2] {'dp'}, use_global_device_ids=true, to_apply=%add | all-reduce | flops 4608 | bytes 36864
  104.6 0.0 copy-done.12
  104.6 0.0 copy-start.7
  104.6 0.1 fusion.11
  104.7 0.0 copy-done.3
  104.7 0.0 copy-done.1
  104.8 0.0 copy-start.5
  104.8 0.5 fusion.4
  105.3 4.3 fusion.19
  109.6 0.0 copy-done.7
  109.6 8.7 %all-reduce.2 = (bf16[320,16]{0,1:T(8,128)(2,1)S(1)}, bf16[320,16]{0,1:T(8,128)(2,1)S(1)}) all-reduce(f32[320,16]{0,1:T(8,128)S(1)} %fusion.19, f32[320,16]{0,1:T(8,128)S(1)} %fusion.4), channel_id=1, replica_groups=mesh['dp'=16,'tensor'=2] {'tensor'}, use_global_device_ids=true, to_apply=%region_1.0 | all-reduce | flops 10240 | bytes 61440 | tf_op jit(solution)/shard_map/psum | solution.py:15
  118.3 0.0 copy-start.9
  118.3 0.0 copy-done.5
  118.3 1.8 convolution_bitcast_fusion.1
  120.2 0.0 reduce-scatter.10.cloned.1.call-update
  120.2 0.0 reduce-scatter.12.cloned.1.call-start
  120.2 0.0 copy-done.9
  120.2 3.7 convolution_bitcast_fusion
  124.0 2.9 copy.17
  126.9 0.0 reduce-scatter.12.cloned.1.call-update
  126.9 0.2 reduce-scatter.8.cloned.1.call-start
  127.1 296.4 %all-gather.4.cloned.1.call-done = bf16[147456,288]{0,1:T(8,128)(2,1)} async-done(((bf16[9216,288]{0,1:T(8,128)(2,1)}), bf16[147456,288]{0,1:T(8,128)(2,1)}) %all-gather.4.cloned.1.call-update) | async-done | bytes 84934672 | tf_op jit(solution)/shard_map/all_gather | solution.py:21
  423.5 0.0 slice-start
  423.5 56.5 %copy.19 = bf16[36,8,16,9216]{3,2,1,0:T(8,128)(2,1)} copy(bf16[36,8,16,9216]{3,1,2,0:T(8,128)(2,1)} %bitcast.12) | data formatting | bytes 169869312
  480.1 0.0 slice-start.1
  480.1 56.8 %copy.13 = bf16[9216,16,288]{0,2,1:T(8,128)(2,1)} copy(bf16[9216,16,288]{0,1,2:T(8,128)(2,1)} %bitcast) | data formatting | bytes 169869312 | tf_op jit(solution)/shard_map/reshape | solution.py:21
  536.8 0.0 slice-done
  536.8 0.0 slice-done.1
  536.8 37.5 %fusion.18 = f32[320,4608]{1,0:T(8,128)} fusion(bf16[320,9216]{1,0:T(8,128)(2,1)S(1)} %bitcast.31, bf16[9216,4608]{0,1:T(8,128)(2,1)} %bitcast.1), kind=kOutput, calls=%fused_computation.24 | convolution fusion | flops 27179089920 | bytes 96731136 | tf_op jit(solution)/shard_map/dot_general | solution.py:23
  574.3 0.0 copy-start.2
  574.3 0.0 copy-start.4
  574.3 0.0 copy-start.6
  574.3 0.0 reduce-scatter.8.cloned.1.call-update
  575.1 0.0 reduce-scatter.10.cloned.1.call-done
  575.1 1.6 copy.16
  576.7 1.7 copy.18
  578.4 70.4 %reduce-scatter.8.cloned.1.call-done = f32[320,2304]{1,0:T(8,128)} async-done(((f32[320,4608]{1,0:T(8,128)}), f32[320,2304]{1,0:T(8,128)}) %reduce-scatter.8.cloned.1.call-update) | async-done | bytes 2949136 | tf_op jit(solution)/shard_map/reduce_scatter | solution.py:30
  648.8 0.0 copy-done.2
  648.8 0.0 copy-done.4
  648.8 0.0 copy-done.6
  648.8 0.0 copy-done.10
  648.9 3.7 fusion.1
  652.5 0.0 copy-done.8
  652.5 0.1 fusion.12
  652.6 61.1 %all-reduce.1 = f32[2304]{0:T(1024)S(1)} all-reduce(f32[2304]{0:T(1024)S(1)} %fusion.12), channel_id=4, replica_groups=mesh['dp'=16,'tensor'=2] {'dp'}, use_global_device_ids=true, to_apply=%region_5.0.clone | all-reduce | flops 2304 | bytes 18432
  713.7 0.6 dynamic-slice.3
  (6 shorter events, 0.0 us)
Async XLA Ops:
  7.2 26.9 %copy-start = (bf16[9216,16]{0,1:T(8,128)(2,1)S(1)}, bf16[9216,16]{0,1:T(8,128)(2,1)}, u32[]{:S(2)}) copy-start(bf16[9216,16]{0,1:T(8,128)(2,1)} %param.8) | copy-start | bytes 884740
  7.2 25.6 %copy-start.13 = (u32[32]{0:T(128)S(1)}, u32[32]{0:T(128)}, u32[]{:S(2)}) copy-start(u32[32]{0:T(128)} %constant.16) | copy-start | bytes 388
  7.2 0.8 copy-start.11
  7.2 416.3 %all-gather.4.cloned.1.call-start = ((), (), s32[]{:S(2)}) async-start(), calls=%async_computation.4 | async-start | bytes 90243072 | tf_op jit(solution)/shard_map/all_gather | solution.py:21
  7.9 567.2 %reduce-scatter.10.cloned.1.call-start = ((), (), s32[]{:S(2)}) async-start(), calls=%async_computation.5 | async-start | bytes 1253376
  32.8 72.0 %copy-start.3 = (bf16[4608,16]{0,1:T(8,128)(2,1)}, bf16[4608,16]{0,1:T(8,128)(2,1)S(1)}, u32[]{:S(2)}) copy-start(bf16[4608,16]{0,1:T(8,128)(2,1)S(1)} %reshape.22) | copy-start | bytes 442372
  34.0 70.6 %copy-start.12 = (f32[2304]{0:T(1024)S(1)}, f32[2304]{0:T(1024)}, u32[]{:S(2)}) copy-start(f32[2304]{0:T(1024)} %param.10) | copy-start | bytes 27652
  34.1 70.7 %copy-start.1 = (bf16[320,2304]{1,0:T(8,128)(2,1)S(1)}, bf16[320,2304]{1,0:T(8,128)(2,1)}, u32[]{:S(2)}) copy-start(bf16[320,2304]{1,0:T(8,128)(2,1)} %param.11) | copy-start | bytes 4423684
  104.6 5.0 copy-start.7
  104.8 13.6 %copy-start.5 = (f32[2304]{0:T(1024)}, f32[2304]{0:T(1024)S(1)}, u32[]{:S(2)}) copy-start(f32[2304]{0:T(1024)S(1)} %fusion.11) | copy-start | bytes 27652
  118.3 1.9 copy-start.9
  120.2 456.5 %reduce-scatter.12.cloned.1.call-start = ((), (), s32[]{:S(2)}) async-start(), calls=%async_computation.6 | async-start | bytes 5013504
  126.9 522.0 %reduce-scatter.8.cloned.1.call-start = ((), (), s32[]{:S(2)}) async-start(), calls=%async_computation.3 | async-start | bytes 8847360 | tf_op jit(solution)/shard_map/reduce_scatter | solution.py:30
  423.5 113.3 %slice-start = ((s8[5898240]{0:T(1024)(128)(4,1)}), s8[4194304]{0:T(1024)(128)(4,1)S(1)}, s32[]{:S(2)}) async-start(s8[5898240]{0:T(1024)(128)(4,1)} %bitcast.30), calls=%async_computation.7 | async-start | bytes 8388608
  480.1 56.8 %slice-start.1 = ((s8[5898240]{0:T(1024)(128)(4,1)}), s8[1703936]{0:T(1024)(128)(4,1)S(1)}, s32[]{:S(2)}) async-start(s8[5898240]{0:T(1024)(128)(4,1)} %bitcast.30), calls=%async_computation.8 | async-start | bytes 3407872
  574.3 74.5 %copy-start.2 = (bf16[320,2304]{1,0:T(8,128)(2,1)S(1)}, bf16[320,2304]{1,0:T(8,128)(2,1)}, u32[]{:S(2)}) copy-start(bf16[320,2304]{1,0:T(8,128)(2,1)} %param.11) | copy-start | bytes 4423684
  574.3 74.5 %copy-start.4 = (bf16[4608,16]{0,1:T(8,128)(2,1)S(1)}, bf16[4608,16]{0,1:T(8,128)(2,1)}, u32[]{:S(2)}) copy-start(bf16[4608,16]{0,1:T(8,128)(2,1)} %copy-done.3) | copy-start | bytes 442372
  574.3 74.5 %copy-start.6 = (f32[2304]{0:T(1024)S(1)}, f32[2304]{0:T(1024)}, u32[]{:S(2)}) copy-start(f32[2304]{0:T(1024)} %copy-done.5) | copy-start | bytes 27652
  574.3 74.5 %copy-start.10 = (bf16[320,16]{0,1:T(8,128)(2,1)S(1)}, bf16[320,16]{0,1:T(8,128)(2,1)}, u32[]{:S(2)}) copy-start(bf16[320,16]{0,1:T(8,128)(2,1)} %copy-done.9) | copy-start | bytes 30724
  578.4 74.1 %copy-start.8 = (f32[4608]{0:T(1024)S(1)}, f32[4608]{0:T(1024)}, u32[]{:S(2)}) copy-start(f32[4608]{0:T(1024)} %copy-done.7) | copy-start | bytes 55300
Sparse Core Ops, SparseCore 0:
  9.6 413.9 all-gather.3
  427.7 58.9 reduce-scatter.9
  490.5 74.6 reduce-scatter.11
  574.5 74.3 reduce-scatter.7
